TPU v7x, 32 devices: a whole 2x2x4 slice. The times are simulated.
32 devices in a mesh: row: 4 (over z), col: 8 (over y, x, core).
Axes of the slice: x: 2, y: 2, z: 4, core: 2. Of those that a mesh axis runs over, the one named last changes fastest.
Arguments:
- grad_terms: bfloat16 [8, 2, 4096, 10240], P('col', None, 'row'), may hold values from -25 to 25, as said below
- row_moment: float32 [2, 4096], P(None, 'row'), may hold values from 0.01 to 3
- col_moment: float32 [2, 10240], P(None, 'col'), may hold values from 0.01 to 1
Outputs:
- update: float32 [2, 4096, 10240], P(None, 'row', 'col')
- new_rows: float32 [2, 4096], P(None, 'row')
- new_cols: float32 [2, 10240], P(None, 'col')
Inputs may be any that keep to these rules, and one draw needn't show every extreme that they name: `grad_terms`: partial gradient terms of the 8 batch shards.
All inputs are finite; a program needn't handle non-finite values.
Results may differ from a plain program's by a relative error of at most 0.0003.
Values sent between devices are 32-bit elements; how exact they have to be, the bound alone decides.
A program may use at most 256 MiB of HBM per device.

v0:
```python
import functools

import jax
import jax.numpy as jnp
from jax import lax
from jax.experimental import pallas as pl
from jax.experimental.pallas import tpu as pltpu
from jax.sharding import PartitionSpec as P

MESH = pl.DeviceIdType.MESH
second_decay = 1.0 - 100.0 ** (-0.8)
tiny_square = 1e-30
LANES = 128
PIECE = 64
CHUNK = 16


def flip(me, r):
    bit = 1
    while bit <= r:
        if r & bit:
            me = me + bit * (1 - 2 * lax.rem(me // bit, 2))
        bit *= 2
    return me


class Plan:
    def __init__(self, n, nz, mats, rows, width):
        bits = [1 << b for b in range(n.bit_length() - 1)]
        self.n, self.nz, self.mats, self.rows, self.width = n, nz, mats, rows, width
        self.orders = (bits, bits[:1] + bits[:0:-1])
        self.stages = len(bits) - 1
        self.first = [r for r in range(n) if not r & bits[0]]
        self.first_bit = bits[0]
        self.kept = []
        self.sent = []
        held = [list(self.first), list(self.first)]
        for s in range(1, self.stages + 1):
            sent = [[r for r in held[h] if r & self.orders[h][s]] for h in (0, 1)]
            held = [[r for r in held[h] if not r & self.orders[h][s]] for h in (0, 1)]
            self.sent.append(sent)
            self.kept.append([list(x) for x in held])
        self.piece = PIECE
        self.pieces = mats * rows // self.piece
        self.blocks = mats * rows // LANES
        L = self.stages
        self.offset = [2 * (L - 1) + 1] + [2 * (L - s) for s in range(1, L + 1)]
        self.acc_slots = self.offset[0] + 4
        self.send_slots = 3
        self.load_slots = 4
        self.recv_slots = [6] * (L - 1) + [4]


def kernel(plan, ff, d, grad_terms, row_moment, col_moment, gradient, row_gain, col_gain, new_rows, new_cols, *scratch):
    n, nz, mats, rows, width = plan.n, plan.nz, plan.mats, plan.rows, plan.width
    L, R, half = plan.stages, plan.piece, plan.piece // 2
    total = mats * rows
    (loaded, to_send, acc, grad, row_part, row_mine, row_all, nr_all, nr_sum, col_sum, w_sum, col_all, nc_all, sq_all,
     load_sem, first_send, first_recv, out_sem, row_send, row_recv, col_send, col_recv, sq_send, sq_recv, *rest) = scratch
    recv, send_sem, recv_sem = rest[:L], rest[L:2 * L], rest[2 * L:3 * L]
    me, my_row = lax.axis_index("col"), lax.axis_index("row")
    everyone = n * nz
    mine = my_row * n + me

    def other(i):
        q = lax.rem(mine + i, everyone)
        return q, {"row": q // n, "col": lax.rem(q, n)}

    def remote(src, dst, send, rcv, target):
        return pltpu.make_async_remote_copy(
            src_ref=src, dst_ref=dst, send_sem=send, recv_sem=rcv, device_id=target, device_id_type=MESH
        )

    def col_device(c):
        return {"row": my_row, "col": c}

    sibling = col_device(flip(me, plan.first_bit))

    def loads(p):
        slot = lax.rem(p, plan.load_slots)
        at = pl.multiple_of(p * R, R)
        out = []
        for r in range(n):
            c = pl.multiple_of(flip(me, r) * width, LANES)
            out.append(
                pltpu.make_async_copy(
                    grad_terms.at[pl.ds(at, R), pl.ds(c, width)], loaded.at[slot, r], load_sem.at[slot, r]
                )
            )
        return out

    def first_copy(p):
        return remote(
            to_send.at[lax.rem(p, plan.send_slots)],
            acc.at[lax.rem(p, plan.acc_slots)],
            first_send.at[lax.rem(p, plan.send_slots)],
            first_recv.at[lax.rem(p, plan.acc_slots)],
            sibling,
        )

    def stage_copies(s, h, p):
        slot = lax.rem(p, plan.recv_slots[s - 1])
        bit = plan.orders[h][s]
        target = col_device(flip(me, bit))
        out = []
        for r in plan.sent[s - 1][h]:
            j = plan.kept[s - 1][h].index(r ^ bit)
            out.append(
                remote(
                    acc.at[lax.rem(p, plan.acc_slots), plan.first.index(r), pl.ds(h * half, half)],
                    recv[s - 1].at[slot, h, j],
                    send_sem[s - 1].at[slot, h, j],
                    recv_sem[s - 1].at[slot, h, j],
                    target,
                )
            )
        return out

    def out_copy(p):
        at = pl.multiple_of(p * R, R)
        return pltpu.make_async_copy(grad.at[pl.ds(at, R)], gradient.at[pl.ds(at, R)], out_sem.at[lax.rem(p, 4)])

    def row_copies(k):
        return [
            remote(row_all.at[k, me], row_all.at[k, me], row_send.at[k, i - 1], row_recv.at[k, me], col_device(flip(me, i)))
            for i in range(1, n)
        ]

    def row_arrivals(k):
        for i in range(1, n):
            c = flip(me, i)
            yield remote(row_all.at[k, c], row_all.at[k, c], row_send.at[k, i - 1], row_recv.at[k, c], col_device(c))

    def z_peer(i):
        return lax.rem(my_row + i, nz)

    def col_copy(m, i):
        return remote(
            col_all.at[m, my_row], col_all.at[m, my_row], col_send.at[m, i - 1], col_recv.at[m, my_row],
            {"row": z_peer(i), "col": me},
        )

    def col_arrival(m, i):
        z = z_peer(i)
        return remote(
            col_all.at[m, z], col_all.at[m, z], col_send.at[m, i - 1], col_recv.at[m, z], {"row": z, "col": me}
        )

    def sq_copy(m, i):
        q, target = other(i)
        return remote(sq_all.at[m, mine], sq_all.at[m, mine], sq_send.at[m, i - 1], sq_recv.at[m, mine], target)

    def sq_arrival(m, i):
        q, target = other(i)
        return remote(sq_all.at[m, q], sq_all.at[m, q], sq_send.at[m, i - 1], sq_recv.at[m, q], target)

    def load_step(p):
        for c in loads(p):
            c.start()

    def send_step(p):
        slot, into = lax.rem(p, plan.load_slots), lax.rem(p, plan.send_slots)

        @pl.when(p >= plan.send_slots)
        def _():
            first_copy(p - plan.send_slots).wait_send()

        for c in loads(p):
            c.wait()

        @pl.loop(0, R // CHUNK)
        def _(i):
            at = pl.ds(pl.multiple_of(i * CHUNK, CHUNK), CHUNK)
            for j, r in enumerate(plan.first):
                to_send[into, j, at] = loaded[slot, r ^ plan.first_bit, at].astype(jnp.float32)

        first_copy(p).start()

    def add_own(p, h, r):
        slot, a = lax.rem(p, plan.load_slots), lax.rem(p, plan.acc_slots)
        j = plan.first.index(r)

        @pl.loop(0, half // CHUNK)
        def _(i):
            at = pl.ds(pl.multiple_of(h * half + i * CHUNK, CHUNK), CHUNK)
            acc[a, j, at] += loaded[slot, r, at].astype(jnp.float32)

    def stage_one(p):
        first_copy(p).wait_recv()
        for group in (plan.sent[0], plan.kept[0]):
            for h in (0, 1):
                for r in group[h]:
                    add_own(p, h, r)
        for s0, s1 in zip(stage_copies(1, 0, p), stage_copies(1, 1, p)):
            s0.start()
            s1.start()

    def add_received(s, h, p):
        slot, a = lax.rem(p, plan.recv_slots[s - 1]), lax.rem(p, plan.acc_slots)
        for k, r in enumerate(plan.kept[s - 1][h]):
            j = plan.first.index(r)

            @pl.loop(0, half // CHUNK)
            def _(i):
                inside = pl.multiple_of(i * CHUNK, CHUNK)
                at = pl.ds(h * half + inside, CHUNK)
                acc[a, j, at] += recv[s - 1][slot, h, k, pl.ds(inside, CHUNK)]

    def stage_later(s, p):
        for h in (0, 1):
            for c in stage_copies(s - 1, h, p):
                c.wait()
            add_received(s - 1, h, p)
        for h in (0, 1):
            for c in stage_copies(s, h, p):
                c.start()

    def matrix_of(p):
        return (p * R) // rows

    def final_step(p):
        slot, a, m = lax.rem(p, plan.recv_slots[L - 1]), lax.rem(p, plan.acc_slots), matrix_of(p)
        for h in (0, 1):
            for c in stage_copies(L, h, p):
                c.wait()

            @pl.loop(0, half // CHUNK)
            def _(i):
                inside = pl.multiple_of(i * CHUNK, CHUNK)
                at = h * half + inside
                g = acc[a, 0, pl.ds(at, CHUNK)] + recv[L - 1][slot, h, 0, pl.ds(inside, CHUNK)]
                grad[pl.ds(p * R + at, CHUNK)] = g
                q = g * g + tiny_square
                lane = q[:, :LANES]
                for j in range(1, width // LANES):
                    lane = lane + q[:, j * LANES:(j + 1) * LANES]
                row_part[pl.ds(pl.multiple_of(lax.rem(p * R, LANES) + at, CHUNK), CHUNK)] = lane
                col_sum[m] += sum(q[8 * j:8 * j + 8] for j in range(CHUNK // 8))

        @pl.when(p >= 4)
        def _():
            out_copy(p - 4).wait()

        out_copy(p).start()

        @pl.when(lax.rem((p + 1) * R, rows) == 0)
        def _():
            col_all[m, my_row] = jnp.sum(col_sum[m], axis=0, keepdims=True)

        @pl.when(lax.rem((p + 1) * R, LANES) == 0)
        def _():
            k = (p * R) // LANES
            row_all[k, me] = jnp.sum(row_part[...].T, axis=0, keepdims=True)
            for c in row_copies(k):
                c.start()

        @pl.when(lax.rem((p + 1) * R, rows) == 0)
        def _():
            for i in range(1, nz):
                col_copy(m, i).start()

    def block_step(k):
        m = (k * LANES) // rows
        for c in row_arrivals(k):
            c.wait_recv()
        full = row_all[k, 0]
        for c in range(1, n):
            full = full + row_all[k, c]
        fresh = second_decay * row_mine[k] + (1.0 - second_decay) * full / ff
        nr_all[k] = fresh
        nr_sum[m] += fresh
        inverse = jnp.broadcast_to(1.0 / fresh, (LANES, LANES)).T
        row_part_inv = inverse

        for i in range(LANES // 8):
            g = grad[pl.ds(pl.multiple_of(k * LANES + 8 * i, 8), 8)]
            q = g * g
            w = row_part_inv[8 * i:8 * i + 8]
            w_sum[m] += jnp.concatenate([q[:, j * LANES:(j + 1) * LANES] * w for j in range(width // LANES)], axis=1)

        for c in row_copies(k):
            c.wait_send()

    def matrix_step(m):
        for i in range(1, nz):
            col_arrival(m, i).wait_recv()
        full = col_all[m, 0]
        for z in range(1, nz):
            full = full + col_all[m, z]
        fresh = second_decay * col_moment_of(m) + (1.0 - second_decay) * full / d
        nc_all[m] = fresh
        w = jnp.sum(w_sum[m], axis=0, keepdims=True) / fresh
        part = w[:, :LANES]
        for j in range(1, width // LANES):
            part = part + w[:, j * LANES:(j + 1) * LANES]
        sq_all[m, mine] = jnp.concatenate([part, nr_sum[m]], axis=1)

        @pl.loop(1, everyone)
        def _(i):
            sq_copy(m, i).start()

        for i in range(1, nz):
            col_copy(m, i).wait_send()

    def col_moment_of(m):
        return nc_all[m]

    def scale_step(m):
        @pl.loop(1, everyone)
        def _(i):
            sq_arrival(m, i).wait_recv()

        both = jnp.sum(sq_all[m], axis=0)
        square = jnp.sum(both[:, :LANES], axis=1, keepdims=True)
        level = jnp.sum(both[:, LANES:], axis=1, keepdims=True) / (n * d)
        clip = jnp.maximum(1.0, jnp.sqrt(square * level / (d * ff)))
        col_gain[pl.ds(m, 1), :] = lax.rsqrt(nc_all[m]) * (jnp.sqrt(level) / clip)
        new_cols[pl.ds(m, 1), :] = nc_all[m]

        @pl.loop(1, everyone)
        def _(i):
            sq_copy(m, i).wait_send()

    o = plan.offset
    for p in range(3):
        load_step(p)
    barrier = pltpu.get_barrier_semaphore()

    @pl.loop(1, everyone)
    def _(i):
        q, target = other(i)
        pl.semaphore_signal(barrier, inc=1, device_id=target, device_id_type=MESH)

    for m in range(mats):
        nc_all[m] = col_moment[m:m + 1, :]
        for k in range(rows // LANES):
            row_mine[m * (rows // LANES) + k] = row_moment[m:m + 1, k * LANES:(k + 1) * LANES]
    nr_sum[...] = jnp.zeros_like(nr_sum)
    col_sum[...] = jnp.zeros_like(col_sum)
    w_sum[...] = jnp.zeros_like(w_sum)
    pl.semaphore_wait(barrier, everyone - 1)

    per_block = LANES // R
    late = 2

    @pl.loop(-o[0], plan.pieces + 1)
    def _(t):
        def run(p, step):
            pl.when(jnp.logical_and(p >= 0, p < plan.pieces))(lambda: step(p))

        run(t + o[1], stage_one)
        for s in range(2, L + 1):
            run(t + o[s], functools.partial(stage_later, s))
        run(t - 1, final_step)
        run(t + o[0], send_step)
        pl.when(jnp.logical_and(t + o[0] + 3 < plan.pieces, t + o[0] >= 0))(lambda: load_step(t + o[0] + 3))
        done = t - 1 - late

        @pl.when(jnp.logical_and(done >= 0, lax.rem(done + 1, per_block) == 0))
        def _():
            k = done // per_block
            block_step(k)
            pl.when(lax.rem((k + 1) * LANES, rows) == 0)(lambda: matrix_step((k * LANES) // rows))

    seen = plan.pieces - 1 - late
    for k in range((seen + 1) // per_block, plan.blocks):
        block_step(k)
        if (k + 1) * LANES % rows == 0:
            matrix_step(k * LANES // rows)
    for m in range(mats):
        for k in range(rows // LANES):
            b = m * (rows // LANES) + k
            new_rows[m:m + 1, k * LANES:(k + 1) * LANES] = nr_all[b]
            row_gain[m:m + 1, k * LANES:(k + 1) * LANES] = lax.rsqrt(nr_all[b])
    for m in range(mats):
        scale_step(m)
    for p in range(plan.pieces - plan.send_slots, plan.pieces):
        first_copy(p).wait_send()
    for p in range(plan.pieces - 4, plan.pieces):
        out_copy(p).wait()


def on_device(n, nz, grad_terms, row_moment, col_moment):
    mats, rows, ff = grad_terms.shape[1:]
    width = ff // n
    d = rows * nz
    plan = Plan(n, nz, mats, rows, width)
    L, R, half, everyone = plan.stages, plan.piece, plan.piece // 2, n * nz
    kept = [len(plan.kept[s][0]) for s in range(L)]
    f32 = jnp.float32
    dma = pltpu.SemaphoreType.DMA
    blocks = plan.blocks
    scratch = [
        pltpu.VMEM((plan.load_slots, n, R, width), grad_terms.dtype),
        pltpu.VMEM((plan.send_slots, n // 2, R, width), f32),
        pltpu.VMEM((plan.acc_slots, n // 2, R, width), f32),
        pltpu.VMEM((mats * rows, width), f32),
        pltpu.VMEM((LANES, LANES), f32),
        pltpu.VMEM((blocks, 1, LANES), f32),
        pltpu.VMEM((blocks, n, 1, LANES), f32),
        pltpu.VMEM((blocks, 1, LANES), f32),
        pltpu.VMEM((mats, 1, LANES), f32),
        pltpu.VMEM((mats, 8, width), f32),
        pltpu.VMEM((mats, 8, width), f32),
        pltpu.VMEM((mats, nz, 1, width), f32),
        pltpu.VMEM((mats, 1, width), f32),
        pltpu.VMEM((mats, everyone, 1, 2 * LANES), f32),
        dma((plan.load_slots, n)),
        dma((plan.send_slots,)),
        dma((plan.acc_slots,)),
        dma((4,)),
        dma((blocks, n - 1)),
        dma((blocks, n)),
        dma((mats, nz - 1)),
        dma((mats, nz)),
        dma((mats, everyone - 1)),
        dma((mats, everyone)),
    ]
    scratch += [pltpu.VMEM((plan.recv_slots[s], 2, kept[s], half, width), f32) for s in range(L)]
    scratch += [dma((plan.recv_slots[s], 2, kept[s])) for s in range(L)] * 2
    vmem, anywhere = pl.BlockSpec(memory_space=pltpu.VMEM), pl.BlockSpec(memory_space=pl.ANY)
    gradient, row_gain, col_gain, new_rows, new_cols = pl.pallas_call(
        functools.partial(kernel, plan, ff, d),
        out_shape=(
            jax.ShapeDtypeStruct((mats * rows, width), f32),
            jax.ShapeDtypeStruct((mats, rows), f32),
            jax.ShapeDtypeStruct((mats, width), f32),
            jax.ShapeDtypeStruct((mats, rows), f32),
            jax.ShapeDtypeStruct((mats, width), f32),
        ),
        in_specs=[anywhere, vmem, vmem],
        out_specs=(anywhere, vmem, vmem, vmem, vmem),
        scratch_shapes=scratch,
        compiler_params=pltpu.CompilerParams(
            collective_id=0, has_side_effects=True, vmem_limit_bytes=56 * 1024 * 1024
        ),
        name="reduce_and_level",
    )(grad_terms.reshape(mats * rows, ff), row_moment, col_moment)
    gradient = gradient.reshape(mats, rows, width)
    update = gradient * row_gain[:, :, None] * col_gain[:, None, :]
    return update, new_rows, new_cols


def solution(mesh):
    n, nz = mesh.shape["col"], mesh.shape["row"]
    return jax.shard_map(
        functools.partial(on_device, n, nz),
        mesh=mesh,
        in_specs=(P("col", None, "row", None), P(None, "row"), P(None, "col")),
        out_specs=(P(None, "row", "col"), P(None, "row"), P(None, "col")),
        check_vma=False,
    )
```

profile of v0, /device:TPU:0, one launch (start us, length us, event | category | flops | bytes accessed | tf_op | source)
XLA Modules:
  0.0 375.1 jit_solution(6218233699427851835)
XLA Ops:
  0.6 364.2 %reduce_and_level.1 = (f32[2048,1280]{1,0:T(8,128)}, f32[2,1024]{1,0:T(2,128)}, f32[2,1280]{1,0:T(2,128)}, f32[2,1024]{1,0:T(2,128)}, f32[2,1280]{1,0:T(2,128)}) custom-call(bf16[2048,10240]{1,0:T(8,128)(2,1)} %bitcast.2, f32[2,1024]{1,0:T(2,128)} %row_moment.1, f32[2,1280]{1,0:T(2,128)} %col_moment.1), custom_call_target="tpu_custom_call" | custom-call | tf_op jit(solution)/shard_map/reduce_and_level/pallas_call | solution.py:422
  364.9 0.0 copy-start.1
  364.9 0.0 copy-start
  364.9 9.0 %multiply_multiply_fusion = f32[2,1024,1280]{2,1,0:T(8,128)} fusion(f32[2,1024,1280]{2,1,0:T(8,128)} %bitcast.3, f32[2,1280]{1,0:T(2,128)} %get-tuple-element.10, f32[2,1024]{1,0:T(2,128)} %get-tuple-element.9), kind=kLoop, calls=%fused_computation | loop fusion | flops 5242880 | bytes 20989952 | tf_op jit(solution)/shard_map/mul | solution.py:440
  373.9 0.0 copy-done.1
  373.9 0.6 copy.8
  374.5 0.0 copy-done
  374.5 0.6 copy.9
Async XLA Ops:
  364.9 9.0 %copy-start.1 = (f32[2,1024]{1,0:T(2,128)S(1)}, f32[2,1024]{1,0:T(2,128)}, u32[]{:S(2)}) copy-start(f32[2,1024]{1,0:T(2,128)} %get-tuple-element.17) | copy-start | bytes 24580
  364.9 9.6 %copy-start = (f32[2,1280]{1,0:T(2,128)S(1)}, f32[2,1280]{1,0:T(2,128)}, u32[]{:S(2)}) copy-start(f32[2,1280]{1,0:T(2,128)} %get-tuple-element.18) | copy-start | bytes 30724
where the time goes:
time: 375 us
  Pallas kernels  364 us (97%)
  other arithmetic  9.01 us (2%)
    pallas_call x1, Pallas kernels, on_device(): pl.pallas_call(functools.partial(kernel, plan, ff, d), out_shape=(jax.Sha...  364 us
    mul x1, other arithmetic, on_device(): update = gradient * row_gain[:, :, None] * col_gain[:, None, :]  9.01 us

commit v1 on v0

v1 whole, which is shorter than its diff:
```python
import functools

import jax
import jax.numpy as jnp
from jax import lax
from jax.experimental import pallas as pl
from jax.experimental.pallas import tpu as pltpu
from jax.sharding import PartitionSpec as P

MESH = pl.DeviceIdType.MESH
second_decay = 1.0 - 100.0 ** (-0.8)
tiny_square = 1e-30
LANES = 128
PIECE = 64
CHUNK = 16


def flip(me, r):
    bit = 1
    while bit <= r:
        if r & bit:
            me = me + bit * (1 - 2 * lax.rem(me // bit, 2))
        bit *= 2
    return me


class Plan:
    def __init__(self, n, nz, mats, rows, width):
        bits = [1 << b for b in range(n.bit_length() - 1)]
        self.n, self.nz, self.mats, self.rows, self.width = n, nz, mats, rows, width
        self.orders = (bits, bits[:1] + bits[:0:-1])
        self.stages = len(bits) - 1
        self.first = [r for r in range(n) if not r & bits[0]]
        self.first_bit = bits[0]
        self.kept = []
        self.sent = []
        held = [list(self.first), list(self.first)]
        for s in range(1, self.stages + 1):
            sent = [[r for r in held[h] if r & self.orders[h][s]] for h in (0, 1)]
            held = [[r for r in held[h] if not r & self.orders[h][s]] for h in (0, 1)]
            self.sent.append(sent)
            self.kept.append([list(x) for x in held])
        self.piece = PIECE
        self.pieces = mats * rows // self.piece
        self.blocks = mats * rows // LANES
        L = self.stages
        self.offset = [2 * (L - 1) + 1] + [2 * (L - s) for s in range(1, L + 1)]
        self.acc_slots = self.offset[0] + 4
        self.send_slots = 3
        self.load_slots = 4
        self.recv_slots = [6] * (L - 1) + [4]


def kernel(plan, ff, d, grad_terms, row_moment, col_moment, grad, col_gain, new_rows, new_cols, *scratch):
    n, nz, mats, rows, width = plan.n, plan.nz, plan.mats, plan.rows, plan.width
    L, R, half = plan.stages, plan.piece, plan.piece // 2
    (loaded, to_send, acc, row_old, col_old, row_part, row_mine, row_all, nr_sum, col_sum, w_sum, col_all, sq_all,
     load_sem, first_send, first_recv, old_sem, row_send, row_recv, col_send, col_recv, sq_send, sq_recv, *rest) = scratch
    recv, send_sem, recv_sem = rest[:L], rest[L:2 * L], rest[2 * L:3 * L]
    me, my_row = lax.axis_index("col"), lax.axis_index("row")
    peer = [flip(me, r) for r in range(n)]
    level = [lax.rem(my_row + i, nz) for i in range(nz)]
    far = [(i, r) for i in range(nz - 1, -1, -1) for r in range(n - 1, -1, -1) if i or r]

    def remote(src, dst, send, rcv, i, r):
        return pltpu.make_async_remote_copy(
            src_ref=src, dst_ref=dst, send_sem=send, recv_sem=rcv,
            device_id={"row": level[i], "col": peer[r]}, device_id_type=MESH,
        )

    def load(p, r):
        slot = lax.rem(p, plan.load_slots)
        at = pl.multiple_of(p * R, R)
        c = pl.multiple_of(peer[r] * width, LANES)
        return pltpu.make_async_copy(
            grad_terms.at[pl.ds(at, R), pl.ds(c, width)], loaded.at[slot, r], load_sem.at[slot, r]
        )

    def first_copy(p, j):
        a, b = lax.rem(p, plan.send_slots), lax.rem(p, plan.acc_slots)
        return remote(to_send.at[a, j], acc.at[b, j], first_send.at[a, j], first_recv.at[b, j], 0, plan.first_bit)

    def stage_copy(s, h, p, r):
        slot = lax.rem(p, plan.recv_slots[s - 1])
        bit = plan.orders[h][s]
        j = plan.kept[s - 1][h].index(r ^ bit)
        return remote(
            acc.at[lax.rem(p, plan.acc_slots), plan.first.index(r), pl.ds(h * half, half)],
            recv[s - 1].at[slot, h, j],
            send_sem[s - 1].at[slot, h, j],
            recv_sem[s - 1].at[slot, h, j],
            0,
            bit,
        )

    def stage_copies(s, h, p):
        return [stage_copy(s, h, p, r) for r in plan.sent[s - 1][h]]

    def row_copy(k, r):
        return remote(row_all.at[k, me], row_all.at[k, me], row_send.at[k, r - 1], row_recv.at[k, me], 0, r)

    def row_arrival(k, r):
        c = peer[r]
        return remote(row_all.at[k, c], row_all.at[k, c], row_send.at[k, r - 1], row_recv.at[k, c], 0, r)

    def col_copy(m, i):
        return remote(col_all.at[m, my_row], col_all.at[m, my_row], col_send.at[m, i - 1], col_recv.at[m, my_row], i, 0)

    def col_arrival(m, i):
        z = level[i]
        return remote(col_all.at[m, z], col_all.at[m, z], col_send.at[m, i - 1], col_recv.at[m, z], i, 0)

    def sq_copy(m, i, r):
        here = sq_all.at[m, my_row, me]
        return remote(here, here, sq_send.at[m, i, r], sq_recv.at[m, my_row, me], i, r)

    def sq_arrival(m, i, r):
        there = sq_all.at[m, level[i], peer[r]]
        return remote(there, there, sq_send.at[m, i, r], sq_recv.at[m, level[i], peer[r]], i, r)

    def load_step(p):
        for r in plan.first:
            load(p, r ^ plan.first_bit).start()
        for r in plan.first:
            load(p, r).start()

    def send_step(p):
        slot, into = lax.rem(p, plan.load_slots), lax.rem(p, plan.send_slots)
        waiting = None
        for j, r in enumerate(plan.first):
            pl.when(p >= plan.send_slots)(lambda: first_copy(p - plan.send_slots, j).wait_send())
            load(p, r ^ plan.first_bit).wait()

            @pl.loop(0, R // CHUNK)
            def _(i):
                at = pl.ds(pl.multiple_of(i * CHUNK, CHUNK), CHUNK)
                to_send[into, j, at] = loaded[slot, r ^ plan.first_bit, at].astype(jnp.float32)

            if waiting is not None:
                waiting.start()
            waiting = first_copy(p, j)
        waiting.start()

    def stage_one(p):
        slot, a = lax.rem(p, plan.load_slots), lax.rem(p, plan.acc_slots)
        waiting = []
        for j, r in enumerate(plan.first):
            load(p, r).wait()
            first_copy(p, j).wait_recv()

            @pl.loop(0, R // CHUNK)
            def _(i):
                at = pl.ds(pl.multiple_of(i * CHUNK, CHUNK), CHUNK)
                acc[a, j, at] += loaded[slot, r, at].astype(jnp.float32)

            for c in waiting:
                c.start()
            waiting = [stage_copy(1, h, p, r) for h in (0, 1) if r in plan.sent[0][h]]
        for c in waiting:
            c.start()

    def add_received(s, h, p):
        slot, a = lax.rem(p, plan.recv_slots[s - 1]), lax.rem(p, plan.acc_slots)
        for k, r in enumerate(plan.kept[s - 1][h]):
            j = plan.first.index(r)

            @pl.loop(0, half // CHUNK)
            def _(i):
                inside = pl.multiple_of(i * CHUNK, CHUNK)
                at = pl.ds(h * half + inside, CHUNK)
                acc[a, j, at] += recv[s - 1][slot, h, k, pl.ds(inside, CHUNK)]

    def stage_later(s, p):
        for h in (0, 1):
            for c in stage_copies(s - 1, h, p):
                c.wait()
            add_received(s - 1, h, p)
        for h in (0, 1):
            for c in stage_copies(s, h, p):
                c.start()

    def final_step(p):
        slot, a, m = lax.rem(p, plan.recv_slots[L - 1]), lax.rem(p, plan.acc_slots), (p * R) // rows
        own = plan.first.index(0)
        for h in (0, 1):
            for c in stage_copies(L, h, p):
                c.wait()

            @pl.loop(0, half // CHUNK)
            def _(i):
                inside = pl.multiple_of(i * CHUNK, CHUNK)
                at = h * half + inside
                g = acc[a, own, pl.ds(at, CHUNK)] + recv[L - 1][slot, h, 0, pl.ds(inside, CHUNK)]
                grad[pl.ds(p * R + at, CHUNK)] = g
                q = g * g + tiny_square
                lane = q[:, :LANES]
                for j in range(1, width // LANES):
                    lane = lane + q[:, j * LANES:(j + 1) * LANES]
                row_part[pl.ds(pl.multiple_of(lax.rem(p * R, LANES) + at, CHUNK), CHUNK)] = lane
                col_sum[m] += sum(q[8 * j:8 * j + 8] for j in range(CHUNK // 8))

        last = lax.rem((p + 1) * R, rows) == 0

        @pl.when(last)
        def _():
            col_all[m, my_row] = jnp.sum(col_sum[m], axis=0, keepdims=True)

        @pl.when(lax.rem((p + 1) * R, LANES) == 0)
        def _():
            k = (p * R) // LANES
            row_all[k, me] = jnp.sum(row_part[...].T, axis=0, keepdims=True)

            @pl.when(last)
            def _():
                for i in range(nz - 1, 0, -1):
                    col_copy(m, i).start()

            for r in range(n - 1, 0, -1):
                row_copy(k, r).start()

    def block_step(k):
        m = (k * LANES) // rows
        for r in range(1, n):
            row_arrival(k, r).wait_recv()
        full = row_all[k, 0]
        for c in range(1, n):
            full = full + row_all[k, c]
        fresh = second_decay * row_mine[k] + (1.0 - second_decay) * full / ff
        row_mine[k] = fresh
        nr_sum[m] += fresh
        gain = jnp.broadcast_to(lax.rsqrt(fresh), (LANES, LANES)).T
        for i in range(LANES // 8):
            at = pl.ds(pl.multiple_of(k * LANES + 8 * i, 8), 8)
            by = gain[8 * i:8 * i + 8]
            for j in range(width // LANES):
                lanes = slice(j * LANES, (j + 1) * LANES)
                y = grad[at, lanes] * by
                grad[at, lanes] = y
                w_sum[m, :, lanes] += y * y
        for r in range(1, n):
            row_copy(k, r).wait_send()

    def matrix_step(m):
        for i in range(1, nz):
            col_arrival(m, i).wait_recv()
        full = col_all[m, 0]
        for z in range(1, nz):
            full = full + col_all[m, z]
        fresh = second_decay * col_old[pl.ds(m, 1), :] + (1.0 - second_decay) * full / d
        new_cols[pl.ds(m, 1), :] = fresh
        w = jnp.sum(w_sum[m], axis=0, keepdims=True) / fresh
        part = w[:, :LANES]
        for j in range(1, width // LANES):
            part = part + w[:, j * LANES:(j + 1) * LANES]
        sq_all[m, my_row, me] = jnp.concatenate([part, nr_sum[m]], axis=1)
        for i, r in far:
            sq_copy(m, i, r).start()
        for i in range(1, nz):
            col_copy(m, i).wait_send()

    def scale_step(m):
        for i, r in far:
            sq_arrival(m, i, r).wait_recv()
        both = jnp.sum(sq_all[m].reshape(nz * n, 1, 2 * LANES), axis=0)
        square = jnp.sum(both[:, :LANES], axis=1, keepdims=True)
        mean = jnp.sum(both[:, LANES:], axis=1, keepdims=True) / (n * d)
        clip = jnp.maximum(1.0, jnp.sqrt(square * mean / (d * ff)))
        col_gain[m:m + 1, :] = lax.rsqrt(new_cols[m:m + 1, :]) * (jnp.sqrt(mean) / clip)
        for i, r in far:
            sq_copy(m, i, r).wait_send()

    old_copies = [
        pltpu.make_async_copy(row_moment, row_old, old_sem.at[0]),
        pltpu.make_async_copy(col_moment, col_old, old_sem.at[1]),
    ]

    def old_step():
        for c in old_copies:
            c.wait()
        for m in range(mats):
            for k in range(rows // LANES):
                row_mine[m * (rows // LANES) + k] = row_old[m:m + 1, k * LANES:(k + 1) * LANES]

    o = plan.offset
    load_step(0)
    barrier = pltpu.get_barrier_semaphore()
    partners = [(i, 0) for i in range(nz - 1, 0, -1)] + [(0, bit) for bit in plan.orders[0]]
    for i, r in partners:
        pl.semaphore_signal(barrier, inc=1, device_id={"row": level[i], "col": peer[r]}, device_id_type=MESH)
    for p in range(1, 3):
        load_step(p)
    for c in old_copies:
        c.start()
    nr_sum[...] = jnp.zeros_like(nr_sum)
    col_sum[...] = jnp.zeros_like(col_sum)
    w_sum[...] = jnp.zeros_like(w_sum)
    pl.semaphore_wait(barrier, len(partners))

    per_block = LANES // R
    late = 2

    @pl.loop(-o[0], plan.pieces + 1)
    def _(t):
        def run(p, step):
            pl.when(jnp.logical_and(p >= 0, p < plan.pieces))(lambda: step(p))

        run(t + o[1], stage_one)
        for s in range(2, L + 1):
            run(t + o[s], functools.partial(stage_later, s))
        run(t - 1, final_step)
        run(t + o[0], send_step)
        pl.when(t + o[0] + 3 < plan.pieces)(lambda: load_step(t + o[0] + 3))
        pl.when(t == 0)(old_step)
        done = t - 1 - late

        @pl.when(jnp.logical_and(done >= 0, lax.rem(done + 1, per_block) == 0))
        def _():
            k = done // per_block
            block_step(k)
            pl.when(lax.rem((k + 1) * LANES, rows) == 0)(lambda: matrix_step((k * LANES) // rows))

    seen = plan.pieces - 1 - late
    for k in range((seen + 1) // per_block, plan.blocks):
        block_step(k)
        if (k + 1) * LANES % rows == 0:
            matrix_step(k * LANES // rows)
    for m in range(mats):
        for k in range(rows // LANES):
            new_rows[m:m + 1, k * LANES:(k + 1) * LANES] = row_mine[m * (rows // LANES) + k]
    for p in range(plan.pieces - plan.send_slots, plan.pieces):
        for j in range(n // 2):
            first_copy(p, j).wait_send()
    for m in range(mats):
        scale_step(m)


def finish(mats, grad, col_gain, rows_in, cols_in, update, new_rows, new_cols, scaled, small_sem, out_sem):
    total = grad.shape[0]
    small = [
        pltpu.make_async_copy(rows_in, new_rows, small_sem.at[0]),
        pltpu.make_async_copy(cols_in, new_cols, small_sem.at[1]),
    ]
    step = LANES
    out = [
        pltpu.make_async_copy(scaled.at[pl.ds(c * step, step)], update.at[pl.ds(c * step, step)], out_sem.at[c])
        for c in range(total // step)
    ]
    for c in range(total // step):
        gain = jnp.broadcast_to(col_gain[c * step * mats // total:c * step * mats // total + 1, :], (8, grad.shape[1]))

        @pl.loop(0, step // 8, unroll=2)
        def _(i):
            at = pl.ds(pl.multiple_of(c * step + i * 8, 8), 8)
            scaled[at] = grad[at] * gain

        out[c].start()
        if c == 0:
            for s in small:
                s.start()
    for s in small + out:
        s.wait()


def on_device(n, nz, grad_terms, row_moment, col_moment):
    mats, rows, ff = grad_terms.shape[1:]
    width = ff // n
    d = rows * nz
    plan = Plan(n, nz, mats, rows, width)
    L, R, half = plan.stages, plan.piece, plan.piece // 2
    kept = [len(plan.kept[s][0]) for s in range(L)]
    f32 = jnp.float32
    dma = pltpu.SemaphoreType.DMA
    blocks, total = plan.blocks, mats * rows
    scratch = [
        pltpu.VMEM((plan.load_slots, n, R, width), grad_terms.dtype),
        pltpu.VMEM((plan.send_slots, n // 2, R, width), f32),
        pltpu.VMEM((plan.acc_slots, n // 2, R, width), f32),
        pltpu.VMEM((mats, rows), f32),
        pltpu.VMEM((mats, width), f32),
        pltpu.VMEM((LANES, LANES), f32),
        pltpu.VMEM((blocks, 1, LANES), f32),
        pltpu.VMEM((blocks, n, 1, LANES), f32),
        pltpu.VMEM((mats, 1, LANES), f32),
        pltpu.VMEM((mats, 8, width), f32),
        pltpu.VMEM((mats, 8, width), f32),
        pltpu.VMEM((mats, nz, 1, width), f32),
        pltpu.VMEM((mats, nz, n, 1, 2 * LANES), f32),
        dma((plan.load_slots, n)),
        dma((plan.send_slots, n // 2)),
        dma((plan.acc_slots, n // 2)),
        dma((2,)),
        dma((blocks, n - 1)),
        dma((blocks, n)),
        dma((mats, nz - 1)),
        dma((mats, nz)),
        dma((mats, nz, n)),
        dma((mats, nz, n)),
    ]
    scratch += [pltpu.VMEM((plan.recv_slots[s], 2, kept[s], half, width), f32) for s in range(L)]
    scratch += [dma((plan.recv_slots[s], 2, kept[s])) for s in range(L)] * 2
    vmem, anywhere = pl.BlockSpec(memory_space=pltpu.VMEM), pl.BlockSpec(memory_space=pl.ANY)
    held = pl.pallas_call(
        functools.partial(kernel, plan, ff, d),
        out_shape=(
            pltpu.VMEM((total, width), f32),
            pltpu.VMEM((mats, width), f32),
            pltpu.VMEM((mats, rows), f32),
            pltpu.VMEM((mats, width), f32),
        ),
        in_specs=[anywhere] * 3,
        out_specs=(vmem,) * 4,
        scratch_shapes=scratch,
        compiler_params=pltpu.CompilerParams(
            collective_id=0, has_side_effects=True, vmem_limit_bytes=44 * 1024 * 1024
        ),
        name="reduce_and_level",
    )(grad_terms.reshape(total, ff), row_moment, col_moment)
    update, new_rows, new_cols = pl.pallas_call(
        functools.partial(finish, mats),
        out_shape=(
            jax.ShapeDtypeStruct((total, width), f32),
            jax.ShapeDtypeStruct((mats, rows), f32),
            jax.ShapeDtypeStruct((mats, width), f32),
        ),
        in_specs=[vmem] * 4,
        out_specs=(anywhere,) * 3,
        scratch_shapes=[pltpu.VMEM((total, width), f32), dma((2,)), dma((total // LANES,))],
        compiler_params=pltpu.CompilerParams(vmem_limit_bytes=24 * 1024 * 1024),
        name="scale_and_write",
    )(*held)
    return update.reshape(mats, rows, width), new_rows, new_cols


def solution(mesh):
    n, nz = mesh.shape["col"], mesh.shape["row"]
    return jax.shard_map(
        functools.partial(on_device, n, nz),
        mesh=mesh,
        in_specs=(P("col", None, "row", None), P(None, "row"), P(None, "col")),
        out_specs=(P(None, "row", "col"), P(None, "row"), P(None, "col")),
        check_vma=False,
    )
```

time: 375 us -> 367 us (0.979)
  other arithmetic: 9.01 us -> 0 us
    mul x1 -> x0, other arithmetic: 9.01 us -> none  [on_device(): update = gradient * row_gain[:, :, None] * col_gain[:, None, :]]
    pallas_call x1 -> x2, Pallas kernels: 364 us -> 366 us  [the longest x1 362 us: on_device(): pl.pallas_call(functools.partial(kernel, plan, ff, d), out_shape=(pltpu.V...]
where the time goes in v1:
time: 367 us; the launch traced here: 366 us
  Pallas kernels  366 us (100%)
    pallas_call x1, Pallas kernels, on_device(): pl.pallas_call(functools.partial(kernel, plan, ff, d), out_shape=(pltpu.V...  362 us

profile of v1, /device:TPU:0, one launch (start us, length us, event | category | flops | bytes accessed | tf_op | source)
XLA Modules:
  0.0 366.4 jit_solution(8123694795721157924)
XLA Ops:
  0.6 361.6 %reduce_and_level.1 = (f32[2048,1280]{1,0:T(8,128)S(1)}, f32[2,1280]{1,0:T(2,128)S(1)}, f32[2,1024]{1,0:T(2,128)S(1)}, f32[2,1280]{1,0:T(2,128)S(1)}) custom-call(bf16[2048,10240]{1,0:T(8,128)(2,1)} %bitcast.2, f32[2,1024]{1,0:T(2,128)} %row_moment.1, f32[2,1280]{1,0:T(2,128)} %col_moment.1), custom_call_target="tpu_custom_call" | custom-call | tf_op jit(solution)/shard_map/reduce_and_level/pallas_call | solution.py:402
  362.2 4.2 %scale_and_write.1 = (f32[2048,1280]{1,0:T(8,128)}, f32[2,1024]{1,0:T(2,128)}, f32[2,1280]{1,0:T(2,128)}) custom-call(f32[2048,1280]{1,0:T(8,128)S(1)} %get-tuple-element.10.grad, f32[2,1280]{1,0:T(2,128)S(1)} %get-tuple-element.11.col_gain, f32[2,1024]{1,0:T(2,128)S(1)} %get-tuple-element.12.rows_in, f32[2,1280]{1,0:T(2,128)S(1)} %get-tuple-element.13.cols_in), custom_call_target="tpu_custom_call" | custom-call | tf_op jit(solution)/shard_map/scale_and_write/pallas_call | solution.py:418

commit v2 on v1

--- a/solution.py
+++ b/solution.py
@@ -40,6 +40,9 @@
             held = [[r for r in held[h] if not r & self.orders[h][s]] for h in (0, 1)]
             self.sent.append(sent)
             self.kept.append([list(x) for x in held])
+        early = [(r, h) for pair in zip(*(self.sent[0][h][::-1] for h in (0, 1))) for h, r in enumerate(pair)]
+        late = [(r, h) for pair in zip(*(self.kept[0][h] for h in (0, 1))) for h, r in enumerate(pair)]
+        self.units = early + late
         self.piece = PIECE
         self.pieces = mats * rows // self.piece
         self.blocks = mats * rows // LANES
@@ -49,6 +52,7 @@
         self.send_slots = 3
         self.load_slots = 4
         self.recv_slots = [6] * (L - 1) + [4]
+        self.row_slots = -(-(self.offset[0] + 4) * self.piece // LANES)
 
 
 def kernel(plan, ff, d, grad_terms, row_moment, col_moment, grad, col_gain, new_rows, new_cols, *scratch):
@@ -72,13 +76,30 @@
         slot = lax.rem(p, plan.load_slots)
         at = pl.multiple_of(p * R, R)
         c = pl.multiple_of(peer[r] * width, LANES)
+        group = int(r not in plan.first)
+        j = plan.first.index(r ^ (group * plan.first_bit))
         return pltpu.make_async_copy(
-            grad_terms.at[pl.ds(at, R), pl.ds(c, width)], loaded.at[slot, r], load_sem.at[slot, r]
+            grad_terms.at[pl.ds(at, R), pl.ds(c, width)],
+            loaded.at[slot, group, j],
+            load_sem.at[slot, group],
         )
 
-    def first_copy(p, j):
-        a, b = lax.rem(p, plan.send_slots), lax.rem(p, plan.acc_slots)
-        return remote(to_send.at[a, j], acc.at[b, j], first_send.at[a, j], first_recv.at[b, j], 0, plan.first_bit)
+    def wait_load(p, group):
+        slot = lax.rem(p, plan.load_slots)
+        both = loaded.at[slot, group]
+        pltpu.make_async_copy(both, both, load_sem.at[slot, group]).wait()
+
+    def first_copy(p, r, h):
+        a, b, j = lax.rem(p, plan.send_slots), lax.rem(p, plan.acc_slots), plan.first.index(r)
+        at = pl.ds(h * half, half)
+        return remote(
+            to_send.at[a, j, at], acc.at[b, j, at], first_send.at[a], first_recv.at[lax.rem(p, 2), j, h],
+            0, plan.first_bit,
+        )
+
+    def wait_first_sent(p):
+        a = lax.rem(p, plan.send_slots)
+        remote(to_send.at[a], to_send.at[a], first_send.at[a], first_recv.at[0, 0, 0], 0, plan.first_bit).wait_send()
 
     def stage_copy(s, h, p, r):
         slot = lax.rem(p, plan.recv_slots[s - 1])
@@ -87,36 +108,39 @@
         return remote(
             acc.at[lax.rem(p, plan.acc_slots), plan.first.index(r), pl.ds(h * half, half)],
             recv[s - 1].at[slot, h, j],
-            send_sem[s - 1].at[slot, h, j],
-            recv_sem[s - 1].at[slot, h, j],
+            send_sem[s - 1].at[slot, h],
+            recv_sem[s - 1].at[slot, h],
             0,
             bit,
         )
 
-    def stage_copies(s, h, p):
-        return [stage_copy(s, h, p, r) for r in plan.sent[s - 1][h]]
+    def wait_stage(s, h, p):
+        slot = lax.rem(p, plan.recv_slots[s - 1])
+        both = recv[s - 1].at[slot, h]
+        remote(both, both, send_sem[s - 1].at[slot, h], recv_sem[s - 1].at[slot, h], 0, plan.orders[h][s]).wait()
 
     def row_copy(k, r):
-        return remote(row_all.at[k, me], row_all.at[k, me], row_send.at[k, r - 1], row_recv.at[k, me], 0, r)
-
-    def row_arrival(k, r):
-        c = peer[r]
-        return remote(row_all.at[k, c], row_all.at[k, c], row_send.at[k, r - 1], row_recv.at[k, c], 0, r)
+        at = lax.rem(k, plan.row_slots)
+        return remote(row_all.at[k, me], row_all.at[k, me], row_send.at[at], row_recv.at[at], 0, r)
+
+    def row_group(k):
+        at, others = lax.rem(k, plan.row_slots), row_all.at[k, pl.ds(0, n - 1)]
+        return remote(others, others, row_send.at[at], row_recv.at[at], 0, 1)
 
     def col_copy(m, i):
-        return remote(col_all.at[m, my_row], col_all.at[m, my_row], col_send.at[m, i - 1], col_recv.at[m, my_row], i, 0)
-
-    def col_arrival(m, i):
-        z = level[i]
-        return remote(col_all.at[m, z], col_all.at[m, z], col_send.at[m, i - 1], col_recv.at[m, z], i, 0)
+        return remote(col_all.at[m, my_row], col_all.at[m, my_row], col_send.at[m], col_recv.at[m], i, 0)
+
+    def col_group(m):
+        others = col_all.at[m, pl.ds(0, nz - 1)]
+        return remote(others, others, col_send.at[m], col_recv.at[m], 1, 0)
 
     def sq_copy(m, i, r):
-        here = sq_all.at[m, my_row, me]
-        return remote(here, here, sq_send.at[m, i, r], sq_recv.at[m, my_row, me], i, r)
-
-    def sq_arrival(m, i, r):
-        there = sq_all.at[m, level[i], peer[r]]
-        return remote(there, there, sq_send.at[m, i, r], sq_recv.at[m, level[i], peer[r]], i, r)
+        here = sq_all.at[m, my_row * n + me]
+        return remote(here, here, sq_send.at[m], sq_recv.at[m], i, r)
+
+    def sq_group(m):
+        others = sq_all.at[m, pl.ds(0, nz * n - 1)]
+        return remote(others, others, sq_send.at[m], sq_recv.at[m], 1, 0)
 
     def load_step(p):
         for r in plan.first:
@@ -126,38 +150,32 @@
 
     def send_step(p):
         slot, into = lax.rem(p, plan.load_slots), lax.rem(p, plan.send_slots)
-        waiting = None
-        for j, r in enumerate(plan.first):
-            pl.when(p >= plan.send_slots)(lambda: first_copy(p - plan.send_slots, j).wait_send())
-            load(p, r ^ plan.first_bit).wait()
-
-            @pl.loop(0, R // CHUNK)
+        pl.when(p >= plan.send_slots)(lambda: wait_first_sent(p - plan.send_slots))
+        wait_load(p, 1)
+        for r, h in plan.units:
+            j = plan.first.index(r)
+
+            @pl.loop(0, half // CHUNK)
             def _(i):
-                at = pl.ds(pl.multiple_of(i * CHUNK, CHUNK), CHUNK)
-                to_send[into, j, at] = loaded[slot, r ^ plan.first_bit, at].astype(jnp.float32)
-
-            if waiting is not None:
-                waiting.start()
-            waiting = first_copy(p, j)
-        waiting.start()
+                at = pl.ds(pl.multiple_of(h * half + i * CHUNK, CHUNK), CHUNK)
+                to_send[into, j, at] = loaded[slot, 1, j, at].astype(jnp.float32)
+
+            first_copy(p, r, h).start()
 
     def stage_one(p):
         slot, a = lax.rem(p, plan.load_slots), lax.rem(p, plan.acc_slots)
-        waiting = []
-        for j, r in enumerate(plan.first):
-            load(p, r).wait()
-            first_copy(p, j).wait_recv()
-
-            @pl.loop(0, R // CHUNK)
+        wait_load(p, 0)
+        for r, h in plan.units:
+            j = plan.first.index(r)
+            first_copy(p, r, h).wait_recv()
+
+            @pl.loop(0, half // CHUNK)
             def _(i):
-                at = pl.ds(pl.multiple_of(i * CHUNK, CHUNK), CHUNK)
-                acc[a, j, at] += loaded[slot, r, at].astype(jnp.float32)
-
-            for c in waiting:
-                c.start()
-            waiting = [stage_copy(1, h, p, r) for h in (0, 1) if r in plan.sent[0][h]]
-        for c in waiting:
-            c.start()
+                at = pl.ds(pl.multiple_of(h * half + i * CHUNK, CHUNK), CHUNK)
+                acc[a, j, at] += loaded[slot, 0, j, at].astype(jnp.float32)
+
+            if r in plan.sent[0][h]:
+                stage_copy(1, h, p, r).start()
 
     def add_received(s, h, p):
         slot, a = lax.rem(p, plan.recv_slots[s - 1]), lax.rem(p, plan.acc_slots)
@@ -172,19 +190,17 @@
 
     def stage_later(s, p):
         for h in (0, 1):
-            for c in stage_copies(s - 1, h, p):
-                c.wait()
+            wait_stage(s - 1, h, p)
             add_received(s - 1, h, p)
         for h in (0, 1):
-            for c in stage_copies(s, h, p):
-                c.start()
+            for r in plan.sent[s - 1][h]:
+                stage_copy(s, h, p, r).start()
 
     def final_step(p):
         slot, a, m = lax.rem(p, plan.recv_slots[L - 1]), lax.rem(p, plan.acc_slots), (p * R) // rows
         own = plan.first.index(0)
         for h in (0, 1):
-            for c in stage_copies(L, h, p):
-                c.wait()
+            wait_stage(L, h, p)
 
             @pl.loop(0, half // CHUNK)
             def _(i):
@@ -220,8 +236,7 @@
 
     def block_step(k):
         m = (k * LANES) // rows
-        for r in range(1, n):
-            row_arrival(k, r).wait_recv()
+        row_group(k).wait_recv()
         full = row_all[k, 0]
         for c in range(1, n):
             full = full + row_all[k, c]
@@ -237,12 +252,10 @@
                 y = grad[at, lanes] * by
                 grad[at, lanes] = y
                 w_sum[m, :, lanes] += y * y
-        for r in range(1, n):
-            row_copy(k, r).wait_send()
+        row_group(k).wait_send()
 
     def matrix_step(m):
-        for i in range(1, nz):
-            col_arrival(m, i).wait_recv()
+        col_group(m).wait_recv()
         full = col_all[m, 0]
         for z in range(1, nz):
             full = full + col_all[m, z]
@@ -252,22 +265,19 @@
         part = w[:, :LANES]
         for j in range(1, width // LANES):
             part = part + w[:, j * LANES:(j + 1) * LANES]
-        sq_all[m, my_row, me] = jnp.concatenate([part, nr_sum[m]], axis=1)
+        sq_all[m, my_row * n + me] = jnp.concatenate([part, nr_sum[m]], axis=1)
         for i, r in far:
             sq_copy(m, i, r).start()
-        for i in range(1, nz):
-            col_copy(m, i).wait_send()
+        col_group(m).wait_send()
 
     def scale_step(m):
-        for i, r in far:
-            sq_arrival(m, i, r).wait_recv()
-        both = jnp.sum(sq_all[m].reshape(nz * n, 1, 2 * LANES), axis=0)
+        sq_group(m).wait_recv()
+        both = jnp.sum(sq_all[m], axis=0)
         square = jnp.sum(both[:, :LANES], axis=1, keepdims=True)
         mean = jnp.sum(both[:, LANES:], axis=1, keepdims=True) / (n * d)
         clip = jnp.maximum(1.0, jnp.sqrt(square * mean / (d * ff)))
         col_gain[m:m + 1, :] = lax.rsqrt(new_cols[m:m + 1, :]) * (jnp.sqrt(mean) / clip)
-        for i, r in far:
-            sq_copy(m, i, r).wait_send()
+        sq_group(m).wait_send()
 
     old_copies = [
         pltpu.make_async_copy(row_moment, row_old, old_sem.at[0]),
@@ -328,8 +338,7 @@
         for k in range(rows // LANES):
             new_rows[m:m + 1, k * LANES:(k + 1) * LANES] = row_mine[m * (rows // LANES) + k]
     for p in range(plan.pieces - plan.send_slots, plan.pieces):
-        for j in range(n // 2):
-            first_copy(p, j).wait_send()
+        wait_first_sent(p)
     for m in range(mats):
         scale_step(m)
 
@@ -342,7 +351,7 @@
     ]
     step = LANES
     out = [
-        pltpu.make_async_copy(scaled.at[pl.ds(c * step, step)], update.at[pl.ds(c * step, step)], out_sem.at[c])
+        pltpu.make_async_copy(scaled.at[pl.ds(c * step, step)], update.at[pl.ds(c * step, step)], out_sem)
         for c in range(total // step)
     ]
     for c in range(total // step):
@@ -357,8 +366,9 @@
         if c == 0:
             for s in small:
                 s.start()
-    for s in small + out:
+    for s in small:
         s.wait()
+    pltpu.make_async_copy(scaled, update, out_sem).wait()
 
 
 def on_device(n, nz, grad_terms, row_moment, col_moment):
@@ -366,13 +376,13 @@
     width = ff // n
     d = rows * nz
     plan = Plan(n, nz, mats, rows, width)
-    L, R, half = plan.stages, plan.piece, plan.piece // 2
+    L, R, half, everyone = plan.stages, plan.piece, plan.piece // 2, n * nz
     kept = [len(plan.kept[s][0]) for s in range(L)]
     f32 = jnp.float32
     dma = pltpu.SemaphoreType.DMA
     blocks, total = plan.blocks, mats * rows
     scratch = [
-        pltpu.VMEM((plan.load_slots, n, R, width), grad_terms.dtype),
+        pltpu.VMEM((plan.load_slots, 2, n // 2, R, width), grad_terms.dtype),
         pltpu.VMEM((plan.send_slots, n // 2, R, width), f32),
         pltpu.VMEM((plan.acc_slots, n // 2, R, width), f32),
         pltpu.VMEM((mats, rows), f32),
@@ -384,20 +394,20 @@
         pltpu.VMEM((mats, 8, width), f32),
         pltpu.VMEM((mats, 8, width), f32),
         pltpu.VMEM((mats, nz, 1, width), f32),
-        pltpu.VMEM((mats, nz, n, 1, 2 * LANES), f32),
-        dma((plan.load_slots, n)),
-        dma((plan.send_slots, n // 2)),
-        dma((plan.acc_slots, n // 2)),
+        pltpu.VMEM((mats, everyone, 1, 2 * LANES), f32),
+        dma((plan.load_slots, 2)),
+        dma((plan.send_slots,)),
+        dma((2, n // 2, 2)),
         dma((2,)),
-        dma((blocks, n - 1)),
-        dma((blocks, n)),
-        dma((mats, nz - 1)),
-        dma((mats, nz)),
-        dma((mats, nz, n)),
-        dma((mats, nz, n)),
+        dma((plan.row_slots,)),
+        dma((plan.row_slots,)),
+        dma((mats,)),
+        dma((mats,)),
+        dma((mats,)),
+        dma((mats,)),
     ]
     scratch += [pltpu.VMEM((plan.recv_slots[s], 2, kept[s], half, width), f32) for s in range(L)]
-    scratch += [dma((plan.recv_slots[s], 2, kept[s])) for s in range(L)] * 2
+    scratch += [dma((plan.recv_slots[s], 2)) for s in range(L)] * 2
     vmem, anywhere = pl.BlockSpec(memory_space=pltpu.VMEM), pl.BlockSpec(memory_space=pl.ANY)
     held = pl.pallas_call(
         functools.partial(kernel, plan, ff, d),
@@ -424,7 +434,7 @@
         ),
         in_specs=[vmem] * 4,
         out_specs=(anywhere,) * 3,
-        scratch_shapes=[pltpu.VMEM((total, width), f32), dma((2,)), dma((total // LANES,))],
+        scratch_shapes=[pltpu.VMEM((total, width), f32), dma((2,)), dma],
         compiler_params=pltpu.CompilerParams(vmem_limit_bytes=24 * 1024 * 1024),
         name="scale_and_write",
     )(*held)

time: 367 us -> 361 us (0.984)
  Pallas kernels: 366 us -> 360 us
    pallas_call x1, Pallas kernels: 362 us -> 356 us  [on_device(): pl.pallas_call(functools.partial(kernel, plan, ff, d), out_shape=(pltpu.V...]
where the time goes in v2:
time: 361 us
  Pallas kernels  360 us (100%)
    pallas_call x1, Pallas kernels, on_device(): pl.pallas_call(functools.partial(kernel, plan, ff, d), out_shape=(pltpu.V...  356 us

profile of v2, /device:TPU:0, one launch (start us, length us, event | category | flops | bytes accessed | tf_op | source)
XLA Modules:
  0.0 360.7 jit_solution(12543946507598552164)
XLA Ops:
  0.6 356.0 %reduce_and_level.1 = (f32[2048,1280]{1,0:T(8,128)S(1)}, f32[2,1280]{1,0:T(2,128)S(1)}, f32[2,1024]{1,0:T(2,128)S(1)}, f32[2,1280]{1,0:T(2,128)S(1)}) custom-call(bf16[2048,10240]{1,0:T(8,128)(2,1)} %bitcast.2, f32[2,1024]{1,0:T(2,128)} %row_moment.1, f32[2,1280]{1,0:T(2,128)} %col_moment.1), custom_call_target="tpu_custom_call" | custom-call | tf_op jit(solution)/shard_map/reduce_and_level/pallas_call | solution.py:412
  356.7 4.0 %scale_and_write.1 = (f32[2048,1280]{1,0:T(8,128)}, f32[2,1024]{1,0:T(2,128)}, f32[2,1280]{1,0:T(2,128)}) custom-call(f32[2048,1280]{1,0:T(8,128)S(1)} %get-tuple-element.10.grad, f32[2,1280]{1,0:T(2,128)S(1)} %get-tuple-element.11.col_gain, f32[2,1024]{1,0:T(2,128)S(1)} %get-tuple-element.12.rows_in, f32[2,1280]{1,0:T(2,128)S(1)} %get-tuple-element.13.cols_in), custom_call_target="tpu_custom_call" | custom-call | tf_op jit(solution)/shard_map/scale_and_write/pallas_call | solution.py:428

commit v3 on v2

--- a/solution.py
+++ b/solution.py
@@ -108,16 +108,16 @@
         return remote(
             acc.at[lax.rem(p, plan.acc_slots), plan.first.index(r), pl.ds(h * half, half)],
             recv[s - 1].at[slot, h, j],
-            send_sem[s - 1].at[slot, h],
-            recv_sem[s - 1].at[slot, h],
+            send_sem[s - 1].at[slot],
+            recv_sem[s - 1].at[slot],
             0,
             bit,
         )
 
-    def wait_stage(s, h, p):
+    def wait_stage(s, p):
         slot = lax.rem(p, plan.recv_slots[s - 1])
-        both = recv[s - 1].at[slot, h]
-        remote(both, both, send_sem[s - 1].at[slot, h], recv_sem[s - 1].at[slot, h], 0, plan.orders[h][s]).wait()
+        both = recv[s - 1].at[slot]
+        remote(both, both, send_sem[s - 1].at[slot], recv_sem[s - 1].at[slot], 0, plan.orders[0][s]).wait()
 
     def row_copy(k, r):
         at = lax.rem(k, plan.row_slots)
@@ -189,8 +189,8 @@
                 acc[a, j, at] += recv[s - 1][slot, h, k, pl.ds(inside, CHUNK)]
 
     def stage_later(s, p):
+        wait_stage(s - 1, p)
         for h in (0, 1):
-            wait_stage(s - 1, h, p)
             add_received(s - 1, h, p)
         for h in (0, 1):
             for r in plan.sent[s - 1][h]:
@@ -199,8 +199,8 @@
     def final_step(p):
         slot, a, m = lax.rem(p, plan.recv_slots[L - 1]), lax.rem(p, plan.acc_slots), (p * R) // rows
         own = plan.first.index(0)
+        wait_stage(L, p)
         for h in (0, 1):
-            wait_stage(L, h, p)
 
             @pl.loop(0, half // CHUNK)
             def _(i):
@@ -220,17 +220,13 @@
         @pl.when(last)
         def _():
             col_all[m, my_row] = jnp.sum(col_sum[m], axis=0, keepdims=True)
+            for i in range(nz - 1, 0, -1):
+                col_copy(m, i).start()
 
         @pl.when(lax.rem((p + 1) * R, LANES) == 0)
         def _():
             k = (p * R) // LANES
             row_all[k, me] = jnp.sum(row_part[...].T, axis=0, keepdims=True)
-
-            @pl.when(last)
-            def _():
-                for i in range(nz - 1, 0, -1):
-                    col_copy(m, i).start()
-
             for r in range(n - 1, 0, -1):
                 row_copy(k, r).start()
 
@@ -349,7 +345,7 @@
         pltpu.make_async_copy(rows_in, new_rows, small_sem.at[0]),
         pltpu.make_async_copy(cols_in, new_cols, small_sem.at[1]),
     ]
-    step = LANES
+    step = LANES // 2
     out = [
         pltpu.make_async_copy(scaled.at[pl.ds(c * step, step)], update.at[pl.ds(c * step, step)], out_sem)
         for c in range(total // step)
@@ -407,7 +403,7 @@
         dma((mats,)),
     ]
     scratch += [pltpu.VMEM((plan.recv_slots[s], 2, kept[s], half, width), f32) for s in range(L)]
-    scratch += [dma((plan.recv_slots[s], 2)) for s in range(L)] * 2
+    scratch += [dma((plan.recv_slots[s],)) for s in range(L)] * 2
     vmem, anywhere = pl.BlockSpec(memory_space=pltpu.VMEM), pl.BlockSpec(memory_space=pl.ANY)
     held = pl.pallas_call(
         functools.partial(kernel, plan, ff, d),

time: 361 us -> 360 us (level)
  no operation moved by 1% of the time
where the time goes in v3:
time: 360 us
  Pallas kernels  360 us (100%)
    pallas_call x1, Pallas kernels, on_device(): pl.pallas_call(functools.partial(kernel, plan, ff, d), out_shape=(pltpu.V...  356 us

profile of v3, /device:TPU:0, one launch (start us, length us, event | category | flops | bytes accessed | tf_op | source)
XLA Modules:
  0.0 360.3 jit_solution(14702217472202188805)
XLA Ops:
  0.6 355.7 %reduce_and_level.1 = (f32[2048,1280]{1,0:T(8,128)S(1)}, f32[2,1280]{1,0:T(2,128)S(1)}, f32[2,1024]{1,0:T(2,128)S(1)}, f32[2,1280]{1,0:T(2,128)S(1)}) custom-call(bf16[2048,10240]{1,0:T(8,128)(2,1)} %bitcast.2, f32[2,1024]{1,0:T(2,128)} %row_moment.1, f32[2,1280]{1,0:T(2,128)} %col_moment.1), custom_call_target="tpu_custom_call" | custom-call | tf_op jit(solution)/shard_map/reduce_and_level/pallas_call | solution.py:408
  356.4 4.0 %scale_and_write.1 = (f32[2048,1280]{1,0:T(8,128)}, f32[2,1024]{1,0:T(2,128)}, f32[2,1280]{1,0:T(2,128)}) custom-call(f32[2048,1280]{1,0:T(8,128)S(1)} %get-tuple-element.10.grad, f32[2,1280]{1,0:T(2,128)S(1)} %get-tuple-element.11.col_gain, f32[2,1024]{1,0:T(2,128)S(1)} %get-tuple-element.12.rows_in, f32[2,1280]{1,0:T(2,128)S(1)} %get-tuple-element.13.cols_in), custom_call_target="tpu_custom_call" | custom-call | tf_op jit(solution)/shard_map/scale_and_write/pallas_call | solution.py:424

commit v4 on v3

--- a/solution.py
+++ b/solution.py
@@ -50,8 +50,9 @@
         self.offset = [2 * (L - 1) + 1] + [2 * (L - s) for s in range(1, L + 1)]
         self.acc_slots = self.offset[0] + 4
         self.send_slots = 3
-        self.load_slots = 4
+        self.load_slots = 3
         self.recv_slots = [6] * (L - 1) + [4]
+        self.flight = lambda s: 3 if s < L else 2
         self.row_slots = -(-(self.offset[0] + 4) * self.piece // LANES)
 
 
@@ -64,7 +65,8 @@
     me, my_row = lax.axis_index("col"), lax.axis_index("row")
     peer = [flip(me, r) for r in range(n)]
     level = [lax.rem(my_row + i, nz) for i in range(nz)]
-    far = [(i, r) for i in range(nz - 1, -1, -1) for r in range(n - 1, -1, -1) if i or r]
+    first_half = lax.broadcasted_iota(jnp.int32, (1, LANES), 1) < LANES // 2
+    far = [(i % nz, r) for i in range(1, nz + 1) for r in range(n - 1, -1, -1) if i < nz or r]
 
     def remote(src, dst, send, rcv, i, r):
         return pltpu.make_async_remote_copy(
@@ -93,13 +95,13 @@
         a, b, j = lax.rem(p, plan.send_slots), lax.rem(p, plan.acc_slots), plan.first.index(r)
         at = pl.ds(h * half, half)
         return remote(
-            to_send.at[a, j, at], acc.at[b, j, at], first_send.at[a], first_recv.at[lax.rem(p, 2), j, h],
+            to_send.at[a, j, at], acc.at[b, j, at], first_send.at[a], first_recv.at[lax.rem(p, 2), min(plan.units.index((r, h)), 2)],
             0, plan.first_bit,
         )
 
     def wait_first_sent(p):
         a = lax.rem(p, plan.send_slots)
-        remote(to_send.at[a], to_send.at[a], first_send.at[a], first_recv.at[0, 0, 0], 0, plan.first_bit).wait_send()
+        remote(to_send.at[a], to_send.at[a], first_send.at[a], first_recv.at[0, 0], 0, plan.first_bit).wait_send()
 
     def stage_copy(s, h, p, r):
         slot = lax.rem(p, plan.recv_slots[s - 1])
@@ -108,7 +110,7 @@
         return remote(
             acc.at[lax.rem(p, plan.acc_slots), plan.first.index(r), pl.ds(h * half, half)],
             recv[s - 1].at[slot, h, j],
-            send_sem[s - 1].at[slot],
+            send_sem[s - 1].at[lax.rem(p, plan.flight(s))],
             recv_sem[s - 1].at[slot],
             0,
             bit,
@@ -117,7 +119,9 @@
     def wait_stage(s, p):
         slot = lax.rem(p, plan.recv_slots[s - 1])
         both = recv[s - 1].at[slot]
-        remote(both, both, send_sem[s - 1].at[slot], recv_sem[s - 1].at[slot], 0, plan.orders[0][s]).wait()
+        remote(
+            both, both, send_sem[s - 1].at[lax.rem(p, plan.flight(s))], recv_sem[s - 1].at[slot], 0, plan.orders[0][s]
+        ).wait()
 
     def row_copy(k, r):
         at = lax.rem(k, plan.row_slots)
@@ -167,7 +171,11 @@
         wait_load(p, 0)
         for r, h in plan.units:
             j = plan.first.index(r)
-            first_copy(p, r, h).wait_recv()
+            if plan.units.index((r, h)) < 2:
+                first_copy(p, r, h).wait_recv()
+            elif plan.units.index((r, h)) == 2:
+                rest = acc.at[a, pl.ds(0, n // 2 - 1)]
+                remote(rest, rest, first_send.at[0], first_recv.at[lax.rem(p, 2), 2], 0, plan.first_bit).wait_recv()
 
             @pl.loop(0, half // CHUNK)
             def _(i):
@@ -261,7 +269,8 @@
         part = w[:, :LANES]
         for j in range(1, width // LANES):
             part = part + w[:, j * LANES:(j + 1) * LANES]
-        sq_all[m, my_row * n + me] = jnp.concatenate([part, nr_sum[m]], axis=1)
+        both = [x + pltpu.roll(x, LANES // 2, 1) for x in (part, nr_sum[m])]
+        sq_all[m, my_row * n + me] = jnp.where(first_half, *both)
         for i, r in far:
             sq_copy(m, i, r).start()
         col_group(m).wait_send()
@@ -269,8 +278,8 @@
     def scale_step(m):
         sq_group(m).wait_recv()
         both = jnp.sum(sq_all[m], axis=0)
-        square = jnp.sum(both[:, :LANES], axis=1, keepdims=True)
-        mean = jnp.sum(both[:, LANES:], axis=1, keepdims=True) / (n * d)
+        square = jnp.sum(jnp.where(first_half, both, 0.0), axis=1, keepdims=True)
+        mean = jnp.sum(jnp.where(first_half, 0.0, both), axis=1, keepdims=True) / (n * d)
         clip = jnp.maximum(1.0, jnp.sqrt(square * mean / (d * ff)))
         col_gain[m:m + 1, :] = lax.rsqrt(new_cols[m:m + 1, :]) * (jnp.sqrt(mean) / clip)
         sq_group(m).wait_send()
@@ -293,8 +302,7 @@
     partners = [(i, 0) for i in range(nz - 1, 0, -1)] + [(0, bit) for bit in plan.orders[0]]
     for i, r in partners:
         pl.semaphore_signal(barrier, inc=1, device_id={"row": level[i], "col": peer[r]}, device_id_type=MESH)
-    for p in range(1, 3):
-        load_step(p)
+    load_step(1)
     for c in old_copies:
         c.start()
     nr_sum[...] = jnp.zeros_like(nr_sum)
@@ -315,7 +323,7 @@
             run(t + o[s], functools.partial(stage_later, s))
         run(t - 1, final_step)
         run(t + o[0], send_step)
-        pl.when(t + o[0] + 3 < plan.pieces)(lambda: load_step(t + o[0] + 3))
+        pl.when(t + o[0] + 2 < plan.pieces)(lambda: load_step(t + o[0] + 2))
         pl.when(t == 0)(old_step)
         done = t - 1 - late
 
@@ -390,10 +398,10 @@
         pltpu.VMEM((mats, 8, width), f32),
         pltpu.VMEM((mats, 8, width), f32),
         pltpu.VMEM((mats, nz, 1, width), f32),
-        pltpu.VMEM((mats, everyone, 1, 2 * LANES), f32),
+        pltpu.VMEM((mats, everyone, 1, LANES), f32),
         dma((plan.load_slots, 2)),
         dma((plan.send_slots,)),
-        dma((2, n // 2, 2)),
+        dma((2, 3)),
         dma((2,)),
         dma((plan.row_slots,)),
         dma((plan.row_slots,)),
@@ -403,7 +411,8 @@
         dma((mats,)),
     ]
     scratch += [pltpu.VMEM((plan.recv_slots[s], 2, kept[s], half, width), f32) for s in range(L)]
-    scratch += [dma((plan.recv_slots[s],)) for s in range(L)] * 2
+    scratch += [dma((plan.flight(s + 1),)) for s in range(L)]
+    scratch += [dma((plan.recv_slots[s],)) for s in range(L)]
     vmem, anywhere = pl.BlockSpec(memory_space=pltpu.VMEM), pl.BlockSpec(memory_space=pl.ANY)
     held = pl.pallas_call(
         functools.partial(kernel, plan, ff, d),

time: 360 us -> 360 us (level)
  no operation moved by 1% of the time
where the time goes in v4:
time: 360 us
  Pallas kernels  359 us (100%)
    pallas_call x1, Pallas kernels, on_device(): pl.pallas_call(functools.partial(kernel, plan, ff, d), out_shape=(pltpu.V...  355 us

profile of v4, /device:TPU:0, one launch (start us, length us, event | category | flops | bytes accessed | tf_op | source)
XLA Modules:
  0.0 359.9 jit_solution(500823749915224982)
XLA Ops:
  0.6 355.3 %reduce_and_level.1 = (f32[2048,1280]{1,0:T(8,128)S(1)}, f32[2,1280]{1,0:T(2,128)S(1)}, f32[2,1024]{1,0:T(2,128)S(1)}, f32[2,1280]{1,0:T(2,128)S(1)}) custom-call(bf16[2048,10240]{1,0:T(8,128)(2,1)} %bitcast.2, f32[2,1024]{1,0:T(2,128)} %row_moment.1, f32[2,1280]{1,0:T(2,128)} %col_moment.1), custom_call_target="tpu_custom_call" | custom-call | tf_op jit(solution)/shard_map/reduce_and_level/pallas_call | solution.py:417
  355.9 4.0 %scale_and_write.1 = (f32[2048,1280]{1,0:T(8,128)}, f32[2,1024]{1,0:T(2,128)}, f32[2,1280]{1,0:T(2,128)}) custom-call(f32[2048,1280]{1,0:T(8,128)S(1)} %get-tuple-element.10.grad, f32[2,1280]{1,0:T(2,128)S(1)} %get-tuple-element.11.col_gain, f32[2,1024]{1,0:T(2,128)S(1)} %get-tuple-element.12.rows_in, f32[2,1280]{1,0:T(2,128)S(1)} %get-tuple-element.13.cols_in), custom_call_target="tpu_custom_call" | custom-call | tf_op jit(solution)/shard_map/scale_and_write/pallas_call | solution.py:433

commit v5 on v4

--- a/solution.py
+++ b/solution.py
@@ -48,7 +48,7 @@
         self.blocks = mats * rows // LANES
         L = self.stages
         self.offset = [2 * (L - 1) + 1] + [2 * (L - s) for s in range(1, L + 1)]
-        self.acc_slots = self.offset[0] + 4
+        self.acc_slots = self.offset[0] + 5
         self.send_slots = 3
         self.load_slots = 3
         self.recv_slots = [6] * (L - 1) + [4]
@@ -265,6 +265,7 @@
             full = full + col_all[m, z]
         fresh = second_decay * col_old[pl.ds(m, 1), :] + (1.0 - second_decay) * full / d
         new_cols[pl.ds(m, 1), :] = fresh
+        col_gain[pl.ds(m, 1), :] = lax.rsqrt(fresh)
         w = jnp.sum(w_sum[m], axis=0, keepdims=True) / fresh
         part = w[:, :LANES]
         for j in range(1, width // LANES):
@@ -281,7 +282,7 @@
         square = jnp.sum(jnp.where(first_half, both, 0.0), axis=1, keepdims=True)
         mean = jnp.sum(jnp.where(first_half, 0.0, both), axis=1, keepdims=True) / (n * d)
         clip = jnp.maximum(1.0, jnp.sqrt(square * mean / (d * ff)))
-        col_gain[m:m + 1, :] = lax.rsqrt(new_cols[m:m + 1, :]) * (jnp.sqrt(mean) / clip)
+        col_gain[m:m + 1, :] = col_gain[m:m + 1, :] * (jnp.sqrt(mean) / clip)
         sq_group(m).wait_send()
 
     old_copies = [
@@ -319,10 +320,10 @@
             pl.when(jnp.logical_and(p >= 0, p < plan.pieces))(lambda: step(p))
 
         run(t + o[1], stage_one)
+        run(t + o[0], send_step)
         for s in range(2, L + 1):
             run(t + o[s], functools.partial(stage_later, s))
         run(t - 1, final_step)
-        run(t + o[0], send_step)
         pl.when(t + o[0] + 2 < plan.pieces)(lambda: load_step(t + o[0] + 2))
         pl.when(t == 0)(old_step)
         done = t - 1 - late

time: 360 us -> 360 us (level)
  no operation moved by 1% of the time
where the time goes in v5:
time: 360 us
  Pallas kernels  359 us (100%)
    pallas_call x1, Pallas kernels, on_device(): pl.pallas_call(functools.partial(kernel, plan, ff, d), out_shape=(pltpu.V...  355 us

profile of v5, /device:TPU:0, one launch (start us, length us, event | category | flops | bytes accessed | tf_op | source)
XLA Modules:
  0.0 359.9 jit_solution(15136544645437431600)
XLA Ops:
  0.6 355.3 %reduce_and_level.1 = (f32[2048,1280]{1,0:T(8,128)S(1)}, f32[2,1280]{1,0:T(2,128)S(1)}, f32[2,1024]{1,0:T(2,128)S(1)}, f32[2,1280]{1,0:T(2,128)S(1)}) custom-call(bf16[2048,10240]{1,0:T(8,128)(2,1)} %bitcast.2, f32[2,1024]{1,0:T(2,128)} %row_moment.1, f32[2,1280]{1,0:T(2,128)} %col_moment.1), custom_call_target="tpu_custom_call" | custom-call | tf_op jit(solution)/shard_map/reduce_and_level/pallas_call | solution.py:418
  355.9 4.0 %scale_and_write.1 = (f32[2048,1280]{1,0:T(8,128)}, f32[2,1024]{1,0:T(2,128)}, f32[2,1280]{1,0:T(2,128)}) custom-call(f32[2048,1280]{1,0:T(8,128)S(1)} %get-tuple-element.10.grad, f32[2,1280]{1,0:T(2,128)S(1)} %get-tuple-element.11.col_gain, f32[2,1024]{1,0:T(2,128)S(1)} %get-tuple-element.12.rows_in, f32[2,1280]{1,0:T(2,128)S(1)} %get-tuple-element.13.cols_in), custom_call_target="tpu_custom_call" | custom-call | tf_op jit(solution)/shard_map/scale_and_write/pallas_call | solution.py:434
